TPU v7x, 32 devices: a whole 2x2x4 slice. The times are simulated.
32 devices in a mesh: dom: 4 (over z), col: 8 (over y, x, core).
Axes of the slice: x: 2, y: 2, z: 4, core: 2. Of those that a mesh axis runs over, the one named last changes fastest.
Arguments:
- rhs_interior: bfloat16 [4, 48, 8192], P('dom', 'col'), may hold values from -6 to 6
- interior_inv: bfloat16 [4, 8192, 8192], P('dom', None, 'col'), may hold values from -0.0625 to 0.0625
- coupling: bfloat16 [4, 8192, 768], P('dom', 'col'), may hold values from -0.0625 to 0.0625
- rhs_interface: bfloat16 [48, 8192], P('col', 'dom'), may hold values from -6 to 6
- block_ids: int32 [4, 6], P('dom'), may hold values from 0 to 63, as said below
- interface_inv: bfloat16 [8192, 8192], P('dom', 'col'), may hold values from -0.0625 to 0.0625
Outputs:
- interior_solution: bfloat16 [4, 48, 8192], P('dom', None, 'col')
- interface_solution: bfloat16 [48, 8192], P('col')
Inputs may be any that keep to these rules, and one draw needn't show every extreme that they name: `block_ids`: each row names 6 different blocks.
All inputs are finite; a program needn't handle non-finite values.
Results may differ from a plain program's by a relative error of at most 0.025.
Values may be sent and summed in bfloat16 or wider, within the bound.
No kernel may reach another device: no remote copies, remote signals or barrier semaphores. Data moves between devices by JAX's collectives and lax.ppermute only.
A program may use at most 64 MiB of HBM per device.

v0:
```python
import jax
import jax.numpy as jnp
from jax import lax
from jax.sharding import PartitionSpec as P

G = 8192
BS = 128


def per_device(rhs_interior, interior_inv, coupling, rhs_interface, block_ids, interface_inv):
    rhs_local = rhs_interior[0]
    inverse = interior_inv[0]
    couple = coupling[0]
    blocks = block_ids[0]
    row_count = rhs_local.shape[0]
    block_count = blocks.shape[0]
    nblocks = G // BS
    onehot = (blocks[:, None] == jnp.arange(nblocks, dtype=jnp.int32)[None, :]).astype(jnp.float32)
    interior_step = jnp.dot(
        lax.all_gather(rhs_local, "col", axis=0, tiled=True),
        inverse,
        preferred_element_type=jnp.float32,
    ).astype(jnp.bfloat16)
    contribution = lax.psum_scatter(
        jnp.dot(interior_step, couple, preferred_element_type=jnp.float32).astype(jnp.bfloat16),
        "col",
        scatter_dimension=0,
        tiled=True,
    ).astype(jnp.float32)
    placed = jnp.einsum(
        "kb,rks->rbs", onehot, contribution.reshape(row_count, block_count, BS)
    ).reshape(row_count, G)
    summed = lax.psum_scatter(
        placed.astype(jnp.bfloat16), "dom", scatter_dimension=1, tiled=True
    ).astype(jnp.float32)
    reduced = (rhs_interface.astype(jnp.float32) - summed).astype(jnp.bfloat16)
    partial_solution = jnp.dot(
        lax.all_gather(reduced, "col", axis=0, tiled=True),
        interface_inv,
        preferred_element_type=jnp.float32,
    )
    column_total = lax.psum(partial_solution.astype(jnp.bfloat16), "dom")
    solution = lax.all_to_all(column_total, "col", split_axis=0, concat_axis=1, tiled=True)
    local_solution = jnp.einsum(
        "kb,rbs->rks",
        onehot.astype(jnp.bfloat16),
        solution.reshape(row_count, nblocks, BS),
        preferred_element_type=jnp.float32,
    )
    local_solution = local_solution.reshape(row_count, block_count * BS).astype(jnp.bfloat16)
    every_solution = lax.all_gather(local_solution, "col", axis=0, tiled=True)
    correction = jnp.einsum("rl,il->ri", every_solution, couple, preferred_element_type=jnp.float32)
    rhs_columns = lax.all_to_all(rhs_local, "col", split_axis=1, concat_axis=0, tiled=True)
    interior_rhs = (rhs_columns.astype(jnp.float32) - correction).astype(jnp.bfloat16)
    result = jnp.dot(
        lax.all_gather(interior_rhs, "col", axis=1, tiled=True),
        inverse,
        preferred_element_type=jnp.float32,
    )
    interior_solution = result.astype(jnp.bfloat16)[None]
    return (interior_solution, solution)


def solution(mesh):
    placed = (
        P("dom", "col", None),
        P("dom", None, "col"),
        P("dom", "col", None),
        P("col", "dom"),
        P("dom", None),
        P("dom", "col"),
    )
    return jax.shard_map(
        per_device,
        mesh=mesh,
        in_specs=placed,
        out_specs=(P("dom", None, "col"), P("col", None)),
        check_vma=False,
    )
```

profile of v0, /device:TPU:0, one launch (start us, length us, event | category | flops | bytes accessed | tf_op | source)
XLA Modules:
  0.0 168.0 jit_solution(9237124908893844768)
XLA Ops:
  7.2 0.0 reduce-scatter.4.cloned.1.call-start
  7.2 1.2 copy.15
  8.4 14.6 %all-gather = bf16[1,48,8192]{2,0,1:T(2,128)(2,1)S(1)} all-gather(bf16[1,6,8192]{2,0,1:T(2,128)(2,1)S(1)} %copy.15), channel_id=2, replica_groups=mesh['dom'=4,'col'=8] {'col'}, dimensions={1}, use_global_device_ids=true | all-gather | bytes 884736 | tf_op jit(solution)/shard_map/all_gather | solution.py:20
  23.0 9.5 %fusion.21 = bf16[48,768]{1,0:T(8,128)(2,1)S(1)} fusion(bf16[1,1024,768]{2,1,0:T(8,128)(2,1)S(1)} %copy-done, bf16[1,8192,1024]{2,1,0:T(8,128)(2,1)} %param.7, bf16[1,48,8192]{2,0,1:T(2,128)(2,1)S(1)} %all-gather), kind=kOutput, calls=%fused_computation.14 | convolution fusion | flops 880889856 | bytes 19210240 | tf_op jit(solution)/shard_map/dot_general | solution.py:25
  32.6 14.5 %fusion = bf16[8,768]{1,0:T(8,128)(2,1)S(1)} fusion(bf16[48,768]{1,0:T(8,128)(2,1)S(1)} %fusion.21), kind=kCustom, calls=%all-reduce-scatter | all-reduce-scatter fusion | flops 49153 | bytes 86528
  47.1 1.3 collective-permute-start
  48.4 2.0 %collective-permute-start.1 = (bf16[6,768]{1,0:T(8,128)(2,1)S(1)}, bf16[6,768]{1,0:T(8,128)(2,1)S(1)}, u32[]{:S(2)}, u32[]{:S(2)}) collective-permute-start(bf16[6,768]{1,0:T(8,128)(2,1)S(1)} %slice), channel_id=1, source_target_pairs={{0,2},{1,3},{2,4},{3,5},{4,6},{5,7},{8,10},{9,11},{10,12},{11,13},... | collective-permute-start | bytes 27656
  50.4 0.6 dynamic-slice.4
  51.7 0.1 collective-permute-done.1
  51.8 0.2 concatenate
  52.1 0.3 fusion.24
  52.4 0.7 copy.25
  53.1 0.0 reduce-scatter.4.cloned.1.call-update
  53.1 0.0 all-reduce.4.cloned.1.call-start
  53.2 23.2 %reduce-scatter.4.cloned.1.call-done = bf16[6,2048]{1,0:T(8,128)(2,1)} async-done(((bf16[6,8192]{1,0:T(8,128)(2,1)}), bf16[6,2048]{1,0:T(8,128)(2,1)}) %reduce-scatter.4.cloned.1.call-update) | async-done | bytes 24592 | tf_op jit(solution)/shard_map/reduce_scatter | solution.py:33
  76.4 0.8 fusion.35
  77.1 9.3 %all-gather.1 = bf16[8,6,2048]{2,1,0:T(8,128)(2,1)S(1)} all-gather(bf16[1,6,2048]{2,1,0:T(8,128)(2,1)S(1)} %fusion.35), channel_id=1, replica_groups=mesh['dom'=4,'col'=8] {'col'}, dimensions={0}, use_global_device_ids=true | all-gather | bytes 221184 | tf_op jit(solution)/shard_map/all_gather | solution.py:38
  86.4 0.1 reshape.30
  86.5 3.0 %convolution_convert_fusion = bf16[48,1024]{1,0:T(8,128)(2,1)S(1)} fusion(bf16[48,2048]{1,0:T(8,128)(2,1)S(1)} %reshape.30, bf16[2048,1024]{1,0:T(8,128)(2,1)} %param.11), kind=kOutput, calls=%fused_computation.12 | convolution fusion | flops 201375744 | bytes 4489216 | tf_op jit(solution)/shard_map/dot_general | solution.py:37
  89.5 0.7 all_to_all.26
  90.2 0.0 all-reduce.4.cloned.1.call-update
  90.2 8.0 %all_to_all.32 = bf16[6,8,1024]{2,0,1:T(8,128)(2,1)S(1)} all-to-all(bf16[6,8,1024]{2,0,1:T(8,128)(2,1)S(1)} %bitcast.65), channel_id=1, replica_groups=mesh['dom'=4,'col'=8] {'col'}, dimensions={1} | all-to-all | bytes 196608 | tf_op jit(solution)/shard_map/all_to_all | solution.py:53
  98.3 24.0 %all-reduce.4.cloned.1.call-done = bf16[8,6,1024]{2,1,0:T(8,128)(2,1)} async-done(((bf16[8,6,1024]{2,1,0:T(8,128)(2,1)}), bf16[8,6,1024]{2,1,0:T(8,128)(2,1)}) %all-reduce.4.cloned.1.call-update) | async-done | bytes 98320 | tf_op jit(solution)/shard_map/psum | solution.py:42
  122.3 3.6 %all-to-all-start.1 = ((bf16[8,6,1024]{2,1,0:T(8,128)(2,1)}), bf16[8,6,1024]{2,1,0:T(8,128)(2,1)S(1)}, u32[]{:S(2)}, u32[]{:S(2)}) async-start(bf16[8,6,1024]{2,1,0:T(8,128)(2,1)} %all-reduce.4.cloned.1.call-done), calls=%async_computation.2 | async-start | bytes 262144 | tf_op jit(solution)/shard_map/all_to_all | solution.py:43
  126.0 5.4 %all-to-all-done.1 = bf16[8,6,1024]{2,1,0:T(8,128)(2,1)S(1)} async-done(((bf16[8,6,1024]{2,1,0:T(8,128)(2,1)}), bf16[8,6,1024]{2,1,0:T(8,128)(2,1)S(1)}, u32[]{:S(2)}, u32[]{:S(2)}) %all-to-all-start.1) | async-done | bytes 98336 | tf_op jit(solution)/shard_map/all_to_all | solution.py:43
  131.4 0.1 copy.16
  131.5 0.2 fusion.28
  131.7 8.3 %all-gather.2 = bf16[8,6,768]{2,1,0:T(8,128)(2,1)S(1)} all-gather(bf16[1,6,768]{2,1,0:T(8,128)(2,1)S(1)} %reshape.31), channel_id=1, replica_groups=mesh['dom'=4,'col'=8] {'col'}, dimensions={0}, use_global_device_ids=true | all-gather | bytes 82944 | tf_op jit(solution)/shard_map/all_gather | solution.py:51
  140.1 0.6 fusion.12
  140.6 10.4 %all_gather.15 = bf16[48,8192]{1,0:T(8,128)(2,1)S(1)} all-gather(bf16[48,1024]{1,0:T(8,128)(2,1)S(1)} %fusion.12), channel_id=1, replica_groups=mesh['dom'=4,'col'=8] {'col'}, dimensions={1}, use_global_device_ids=true | all-gather | bytes 884736 | tf_op jit(solution)/shard_map/all_gather | solution.py:56
  151.0 9.5 %fusion.25 = bf16[1,48,1024]{2,1,0:T(8,128)(2,1)} fusion(bf16[48,8192]{1,0:T(8,128)(2,1)S(1)} %all_gather.15, bf16[1,8192,1024]{2,1,0:T(8,128)(2,1)} %param.7), kind=kOutput, calls=%fused_computation.16 | convolution fusion | flops 805355520 | bytes 17661952 | tf_op jit(solution)/shard_map/dot_general | solution.py:55
  160.5 0.7 copy.28
  (19 shorter events, 0.2 us)
Async XLA Ops:
  7.2 15.9 %copy-start = (bf16[1,1024,768]{2,1,0:T(8,128)(2,1)S(1)}, bf16[1,1024,768]{2,1,0:T(8,128)(2,1)}, u32[]{:S(2)}) copy-start(bf16[1,1024,768]{2,1,0:T(8,128)(2,1)} %param.8) | copy-start | bytes 4718596
  7.2 69.2 %reduce-scatter.4.cloned.1.call-start = ((), (), s32[]{:S(2)}) async-start(), calls=%async_computation.3 | async-start | bytes 163840 | tf_op jit(solution)/shard_map/reduce_scatter | solution.py:33
  23.0 27.4 %copy-start.3 = (u32[32]{0:T(128)S(1)}, u32[32]{0:T(128)}, u32[]{:S(2)}) copy-start(u32[32]{0:T(128)} %constant.7) | copy-start | bytes 388
  23.0 29.0 %copy-start.4 = (s32[1,6]{1,0:T(1,128)S(1)}, s32[1,6]{1,0:T(1,128)}, u32[]{:S(2)}) copy-start(s32[1,6]{1,0:T(1,128)} %param.10) | copy-start | bytes 76
  23.0 53.3 %copy-start.2 = (bf16[6,2048]{1,0:T(8,128)(2,1)S(1)}, bf16[6,2048]{1,0:T(8,128)(2,1)}, u32[]{:S(2)}) copy-start(bf16[6,2048]{1,0:T(8,128)(2,1)} %param.9) | copy-start | bytes 73732
  32.6 57.6 %copy-start.1 = (bf16[1,6,8192]{2,1,0:T(8,128)(2,1)S(1)}, bf16[1,6,8192]{2,1,0:T(8,128)(2,1)}, u32[]{:S(2)}) copy-start(bf16[1,6,8192]{2,1,0:T(8,128)(2,1)} %param.6) | copy-start | bytes 294916
  47.1 4.7 %collective-permute-start = (bf16[8,768]{1,0:T(8,128)(2,1)S(1)}, bf16[8,768]{1,0:T(8,128)(2,1)S(1)}, u32[]{:S(2)}, u32[]{:S(2)}) collective-permute-start(bf16[8,768]{1,0:T(8,128)(2,1)S(1)} %fusion), channel_id=1, source_target_pairs={{0,1},{1,2},{2,3},{3,4},{4,5},{5,6},{6,7},{8,9},{9,10},{10,11},{11... | collective-permute-start | bytes 36872
  48.4 3.4 %collective-permute-start.1 = (bf16[6,768]{1,0:T(8,128)(2,1)S(1)}, bf16[6,768]{1,0:T(8,128)(2,1)S(1)}, u32[]{:S(2)}, u32[]{:S(2)}) collective-permute-start(bf16[6,768]{1,0:T(8,128)(2,1)S(1)} %slice), channel_id=1, source_target_pairs={{0,2},{1,3},{2,4},{3,5},{4,6},{5,7},{8,10},{9,11},{10,12},{11,13},... | collective-permute-start | bytes 27656
  53.1 69.1 %all-reduce.4.cloned.1.call-start = ((), (), s32[]{:S(2)}) async-start(), calls=%async_computation.4 | async-start | bytes 262144 | tf_op jit(solution)/shard_map/psum | solution.py:42
  122.3 9.1 %all-to-all-start.1 = ((bf16[8,6,1024]{2,1,0:T(8,128)(2,1)}), bf16[8,6,1024]{2,1,0:T(8,128)(2,1)S(1)}, u32[]{:S(2)}, u32[]{:S(2)}) async-start(bf16[8,6,1024]{2,1,0:T(8,128)(2,1)} %all-reduce.4.cloned.1.call-done), calls=%async_computation.2 | async-start | bytes 262144 | tf_op jit(solution)/shard_map/all_to_all | solution.py:43
Sparse Core Ops, SparseCore 0:
  53.3 23.0 reduce-scatter.3
  90.3 31.8 all-reduce.3
where the time goes:
time: 169 us; the launch traced here: 168 us
  blocking collectives  65 us (38%)
  waiting for transfers between devices  52.8 us (31%)
  matrix products  23.1 us (14%)
  between operations  14.9 us (9%)
  starting transfers between devices  7.03 us (4%)
  local copies, waits for them, and re-layouts  4.39 us (3%)
    psum x1, waiting for transfers between devices, per_device(): column_total = lax.psum(partial_solution.astype(jnp.bfloat16), 'dom')  24 us
    reduce_scatter x1, waiting for transfers between devices, per_device(): lax.psum_scatter(placed.astype(jnp.bfloat16), 'dom', scatter_dimension=1,...  23.2 us
    all_gather x1, blocking collectives, per_device(): lax.all_gather(rhs_local, 'col', axis=0, tiled=True)  14.6 us
    unnamed x1, blocking collectives  14.5 us
    all_gather x1, blocking collectives, per_device(): lax.all_gather(interior_rhs, 'col', axis=1, tiled=True)  10.4 us
    dot_general x1, matrix products, per_device(): jnp.dot(interior_step, couple, preferred_element_type=jnp.float32)  9.54 us
    dot_general x1, matrix products, per_device(): jnp.dot(lax.all_gather(interior_rhs, 'col', axis=1, tiled=True), inverse,...  9.46 us
    all_gather x1, blocking collectives, per_device(): lax.all_gather(reduced, 'col', axis=0, tiled=True)  9.25 us
  transfers between devices with their start and end apart: 5, of which 4 were waited for; matrix products, arithmetic and copies ran while one was open for 0% of the time, Pallas kernels for 0%

commit v1 on v0

--- a/solution.py
+++ b/solution.py
@@ -5,6 +5,11 @@
 
 G = 8192
 BS = 128
+
+
+def gather_and_add(array, name):
+    shards = lax.all_gather(array, name)
+    return jnp.sum(shards, axis=0)
 
 
 def per_device(rhs_interior, interior_inv, coupling, rhs_interface, block_ids, interface_inv):
@@ -39,7 +44,7 @@
         interface_inv,
         preferred_element_type=jnp.float32,
     )
-    column_total = lax.psum(partial_solution.astype(jnp.bfloat16), "dom")
+    column_total = gather_and_add(partial_solution.astype(jnp.bfloat16), "dom")
     solution = lax.all_to_all(column_total, "col", split_axis=0, concat_axis=1, tiled=True)
     local_solution = jnp.einsum(
         "kb,rbs->rks",

time: 169 us -> 151 us (0.89)
  waiting for transfers between devices: 52.8 us -> 22.6 us
  blocking collectives: 65 us -> 72.2 us
  starting transfers between devices: 7.03 us -> 12.8 us
    psum x1 -> x0, waiting for transfers between devices: 24 us -> none  [per_device(): column_total = lax.psum(partial_solution.astype(jnp.bfloat16), 'dom')]
    all_gather x0 -> x1, blocking collectives: none -> 15.4 us  [gather_and_add(): shards = lax.all_gather(array, name)]
    all_to_all x1 -> x0, blocking collectives: 8.04 us -> none  [per_device(): lax.all_to_all(rhs_local, 'col', split_axis=1, concat_axis=0, tiled=True)]
    all_to_all x0 -> x1, starting transfers between devices: none -> 6.11 us  [per_device(): lax.all_to_all(rhs_local, 'col', split_axis=1, concat_axis=0, tiled=True)]
    reduce_scatter x1, waiting for transfers between devices: 23.2 us -> 17.1 us  [per_device(): lax.psum_scatter(placed.astype(jnp.bfloat16), 'dom', scatter_dimension=1,...]
    unnamed x20 -> x18, local copies, waits for them, and re-layouts: 3.53 us -> 3.52 us
  transfers between devices with their start and end apart: 5 -> 5, of which waited for: 4 -> 3; matrix products, arithmetic and copies ran while one was open for 0% -> 3% of each run, Pallas kernels for 0% -> 0%
where the time goes in v1:
time: 151 us
  blocking collectives  72.2 us (48%)
  matrix products  23.1 us (15%)
  waiting for transfers between devices  22.6 us (15%)
  between operations  14.8 us (10%)
  starting transfers between devices  12.8 us (8%)
  local copies, waits for them, and re-layouts  4.38 us (3%)
    reduce_scatter x1, waiting for transfers between devices, per_device(): lax.psum_scatter(placed.astype(jnp.bfloat16), 'dom', scatter_dimension=1,...  17.1 us
    all_gather x1, blocking collectives, gather_and_add(): shards = lax.all_gather(array, name)  15.4 us
    all_gather x1, blocking collectives, per_device(): lax.all_gather(rhs_local, 'col', axis=0, tiled=True)  14.6 us
    unnamed x1, blocking collectives  14.3 us
    all_gather x1, blocking collectives, per_device(): lax.all_gather(interior_rhs, 'col', axis=1, tiled=True)  10.4 us
    dot_general x1, matrix products, per_device(): jnp.dot(interior_step, couple, preferred_element_type=jnp.float32)  9.54 us
    dot_general x1, matrix products, per_device(): jnp.dot(lax.all_gather(interior_rhs, 'col', axis=1, tiled=True), inverse,...  9.46 us
    all_gather x1, blocking collectives, per_device(): lax.all_gather(reduced, 'col', axis=0, tiled=True)  9.25 us
  transfers between devices with their start and end apart: 5, of which 3 were waited for; matrix products, arithmetic and copies ran while one was open for 3% of the time, Pallas kernels for 0%

profile of v1, /device:TPU:0, one launch (start us, length us, event | category | flops | bytes accessed | tf_op | source)
XLA Modules:
  0.0 150.8 jit_solution(17846333750220462374)
XLA Ops:
  7.2 0.0 copy-start
  7.2 0.0 reduce-scatter.4.cloned.1.call-start
  7.2 1.2 copy.14
  8.4 14.6 %all-gather = bf16[1,48,8192]{2,0,1:T(2,128)(2,1)S(1)} all-gather(bf16[1,6,8192]{2,0,1:T(2,128)(2,1)S(1)} %copy.14), channel_id=2, replica_groups=mesh['dom'=4,'col'=8] {'col'}, dimensions={1}, use_global_device_ids=true | all-gather | bytes 884736 | tf_op jit(solution)/shard_map/all_gather | solution.py:25
  23.0 9.5 %fusion.21 = bf16[48,768]{1,0:T(8,128)(2,1)S(1)} fusion(bf16[1,1024,768]{2,1,0:T(8,128)(2,1)S(1)} %copy-done, bf16[1,8192,1024]{2,1,0:T(8,128)(2,1)} %param.7, bf16[1,48,8192]{2,0,1:T(2,128)(2,1)S(1)} %all-gather), kind=kOutput, calls=%fused_computation.14 | convolution fusion | flops 880889856 | bytes 19210240 | tf_op jit(solution)/shard_map/dot_general | solution.py:30
  32.6 14.3 %fusion = bf16[8,768]{1,0:T(8,128)(2,1)S(1)} fusion(bf16[48,768]{1,0:T(8,128)(2,1)S(1)} %fusion.21), kind=kCustom, calls=%all-reduce-scatter | all-reduce-scatter fusion | flops 49153 | bytes 86528
  46.9 1.3 collective-permute-start
  48.2 2.0 %collective-permute-start.1 = (bf16[6,768]{1,0:T(8,128)(2,1)S(1)}, bf16[6,768]{1,0:T(8,128)(2,1)S(1)}, u32[]{:S(2)}, u32[]{:S(2)}) collective-permute-start(bf16[6,768]{1,0:T(8,128)(2,1)S(1)} %slice), channel_id=1, source_target_pairs={{0,2},{1,3},{2,4},{3,5},{4,6},{5,7},{8,10},{9,11},{10,12},{11,13},... | collective-permute-start | bytes 27656
  50.3 0.6 dynamic-slice.4
  51.5 0.1 collective-permute-done.1
  51.7 0.2 concatenate
  51.9 0.3 fusion.24
  52.2 0.7 copy.24
  53.0 0.0 reduce-scatter.4.cloned.1.call-update
  53.0 6.1 %all-to-all-start = ((bf16[6,8,1024]{2,0,1:T(8,128)(2,1)}), bf16[6,8,1024]{2,0,1:T(8,128)(2,1)S(1)}, u32[]{:S(2)}, u32[]{:S(2)}) async-start(bf16[6,8,1024]{2,0,1:T(8,128)(2,1)} %bitcast), calls=%async_computation | async-start | bytes 262144 | tf_op jit(solution)/shard_map/all_to_all | solution.py:58
  59.1 17.1 %reduce-scatter.4.cloned.1.call-done = bf16[6,2048]{1,0:T(8,128)(2,1)} async-done(((bf16[6,8192]{1,0:T(8,128)(2,1)}), bf16[6,2048]{1,0:T(8,128)(2,1)}) %reduce-scatter.4.cloned.1.call-update) | async-done | bytes 24592 | tf_op jit(solution)/shard_map/reduce_scatter | solution.py:38
  76.2 0.8 fusion.35
  77.0 9.3 %all-gather.2 = bf16[8,6,2048]{2,1,0:T(8,128)(2,1)S(1)} all-gather(bf16[1,6,2048]{2,1,0:T(8,128)(2,1)S(1)} %fusion.35), channel_id=1, replica_groups=mesh['dom'=4,'col'=8] {'col'}, dimensions={0}, use_global_device_ids=true | all-gather | bytes 221184 | tf_op jit(solution)/shard_map/all_gather | solution.py:43
  86.2 0.1 reshape.31
  86.3 3.0 %convolution_convert_fusion = bf16[48,1024]{1,0:T(8,128)(2,1)S(1)} fusion(bf16[48,2048]{1,0:T(8,128)(2,1)S(1)} %reshape.31, bf16[2048,1024]{1,0:T(8,128)(2,1)} %param.11), kind=kOutput, calls=%fused_computation.12 | convolution fusion | flops 201375744 | bytes 4489216 | tf_op jit(solution)/shard_map/dot_general | solution.py:42
  89.3 15.4 %all-gather.1 = bf16[192,1024]{1,0:T(8,128)(2,1)S(1)} all-gather(bf16[48,1024]{1,0:T(8,128)(2,1)S(1)} %convolution_convert_fusion), channel_id=3, replica_groups=mesh['dom'=4,'col'=8] {'dom'}, dimensions={0}, use_global_device_ids=true | all-gather | bytes 491520 | tf_op jit(solution)/shard_map/all_gather | solution.py:11
  104.7 0.1 reduce_sum.12
  104.8 0.7 all_to_all.26
  105.5 3.4 %all-to-all-start.1 = ((bf16[8,6,1024]{2,1,0:T(8,128)(2,1)}), bf16[8,6,1024]{2,1,0:T(8,128)(2,1)S(1)}, u32[]{:S(2)}, u32[]{:S(2)}) async-start(bf16[8,6,1024]{2,1,0:T(8,128)(2,1)} %all_to_all.26), calls=%async_computation.2 | async-start | bytes 262144 | tf_op jit(solution)/shard_map/all_to_all | solution.py:48
  108.9 5.4 %all-to-all-done.1 = bf16[8,6,1024]{2,1,0:T(8,128)(2,1)S(1)} async-done(((bf16[8,6,1024]{2,1,0:T(8,128)(2,1)}), bf16[8,6,1024]{2,1,0:T(8,128)(2,1)S(1)}, u32[]{:S(2)}, u32[]{:S(2)}) %all-to-all-start.1) | async-done | bytes 98336 | tf_op jit(solution)/shard_map/all_to_all | solution.py:48
  114.3 0.1 copy.15
  114.4 0.2 fusion.28
  114.6 8.3 %all-gather.3 = bf16[8,6,768]{2,1,0:T(8,128)(2,1)S(1)} all-gather(bf16[1,6,768]{2,1,0:T(8,128)(2,1)S(1)} %reshape.32), channel_id=1, replica_groups=mesh['dom'=4,'col'=8] {'col'}, dimensions={0}, use_global_device_ids=true | all-gather | bytes 82944 | tf_op jit(solution)/shard_map/all_gather | solution.py:56
  122.9 0.6 fusion.12
  123.5 10.4 %all_gather.23 = bf16[48,8192]{1,0:T(8,128)(2,1)S(1)} all-gather(bf16[48,1024]{1,0:T(8,128)(2,1)S(1)} %fusion.12), channel_id=1, replica_groups=mesh['dom'=4,'col'=8] {'col'}, dimensions={1}, use_global_device_ids=true | all-gather | bytes 884736 | tf_op jit(solution)/shard_map/all_gather | solution.py:61
  133.9 9.5 %fusion.25 = bf16[1,48,1024]{2,1,0:T(8,128)(2,1)} fusion(bf16[48,8192]{1,0:T(8,128)(2,1)S(1)} %all_gather.23, bf16[1,8192,1024]{2,1,0:T(8,128)(2,1)} %param.7), kind=kOutput, calls=%fused_computation.16 | convolution fusion | flops 805355520 | bytes 17661952 | tf_op jit(solution)/shard_map/dot_general | solution.py:60
  143.3 0.7 copy.26
  (17 shorter events, 0.2 us)
Async XLA Ops:
  7.2 15.9 %copy-start = (bf16[1,1024,768]{2,1,0:T(8,128)(2,1)S(1)}, bf16[1,1024,768]{2,1,0:T(8,128)(2,1)}, u32[]{:S(2)}) copy-start(bf16[1,1024,768]{2,1,0:T(8,128)(2,1)} %param.8) | copy-start | bytes 4718596
  7.2 69.0 %reduce-scatter.4.cloned.1.call-start = ((), (), s32[]{:S(2)}) async-start(), calls=%async_computation.3 | async-start | bytes 163840 | tf_op jit(solution)/shard_map/reduce_scatter | solution.py:38
  23.0 27.2 %copy-start.2 = (u32[32]{0:T(128)S(1)}, u32[32]{0:T(128)}, u32[]{:S(2)}) copy-start(u32[32]{0:T(128)} %constant.10) | copy-start | bytes 388
  23.0 28.9 %copy-start.3 = (s32[1,6]{1,0:T(1,128)S(1)}, s32[1,6]{1,0:T(1,128)}, u32[]{:S(2)}) copy-start(s32[1,6]{1,0:T(1,128)} %param.10) | copy-start | bytes 76
  23.0 53.2 %copy-start.1 = (bf16[6,2048]{1,0:T(8,128)(2,1)S(1)}, bf16[6,2048]{1,0:T(8,128)(2,1)}, u32[]{:S(2)}) copy-start(bf16[6,2048]{1,0:T(8,128)(2,1)} %param.9) | copy-start | bytes 73732
  46.9 4.7 %collective-permute-start = (bf16[8,768]{1,0:T(8,128)(2,1)S(1)}, bf16[8,768]{1,0:T(8,128)(2,1)S(1)}, u32[]{:S(2)}, u32[]{:S(2)}) collective-permute-start(bf16[8,768]{1,0:T(8,128)(2,1)S(1)} %fusion), channel_id=1, source_target_pairs={{0,1},{1,2},{2,3},{3,4},{4,5},{5,6},{6,7},{8,9},{9,10},{10,11},{11... | collective-permute-start | bytes 36872
  48.2 3.4 %collective-permute-start.1 = (bf16[6,768]{1,0:T(8,128)(2,1)S(1)}, bf16[6,768]{1,0:T(8,128)(2,1)S(1)}, u32[]{:S(2)}, u32[]{:S(2)}) collective-permute-start(bf16[6,768]{1,0:T(8,128)(2,1)S(1)} %slice), channel_id=1, source_target_pairs={{0,2},{1,3},{2,4},{3,5},{4,6},{5,7},{8,10},{9,11},{10,12},{11,13},... | collective-permute-start | bytes 27656
  53.0 52.5 %all-to-all-start = ((bf16[6,8,1024]{2,0,1:T(8,128)(2,1)}), bf16[6,8,1024]{2,0,1:T(8,128)(2,1)S(1)}, u32[]{:S(2)}, u32[]{:S(2)}) async-start(bf16[6,8,1024]{2,0,1:T(8,128)(2,1)} %bitcast), calls=%async_computation | async-start | bytes 262144 | tf_op jit(solution)/shard_map/all_to_all | solution.py:58
  105.5 8.8 %all-to-all-start.1 = ((bf16[8,6,1024]{2,1,0:T(8,128)(2,1)}), bf16[8,6,1024]{2,1,0:T(8,128)(2,1)S(1)}, u32[]{:S(2)}, u32[]{:S(2)}) async-start(bf16[8,6,1024]{2,1,0:T(8,128)(2,1)} %all_to_all.26), calls=%async_computation.2 | async-start | bytes 262144 | tf_op jit(solution)/shard_map/all_to_all | solution.py:48
Sparse Core Ops, SparseCore 0:
  53.1 23.0 reduce-scatter.3
